TPU v7x, 256 devices: a whole 4x4x8 slice. The times are simulated.
256 devices in a mesh: grp: 16 (over x, z_lo, core), dev: 16 (over z_hi, y).
Axes of the slice: x: 4, y: 4, z: 8 (z_hi: 4, z_lo: 2; z = z_hi * 2 + z_lo), core: 2. Of those that a mesh axis runs over, the one named last changes fastest.
Arguments:
- a_tiles: float32 [8192, 3, 128, 128], P(('grp', 'dev')), may hold values from -1.7071068 to 18.707107
- prolong: float32 [8192, 2, 128, 128], P(('grp', 'dev')), may hold values from -0.5 to 0.5
- coarse_ids: int32 [8192, 2], P(('grp', 'dev')), may hold values from 0 to 3, as said below
Outputs:
- coarse: float32 [8192, 1536], P(('grp', 'dev'))
Inputs may be any that keep to these rules, and one draw needn't show every extreme that they name: `coarse_ids`: each fine block names 2 different coarse tiles, numbered within its own group.
All inputs are finite; a program needn't handle non-finite values.
Results may differ from a plain program's by a relative error of at most 0.0001.
Values sent between devices are 32-bit elements; how exact they have to be, the bound alone decides.
A program may use at most 128 MiB of HBM per device.

v0:
```python
import jax
import jax.numpy as jnp
from jax import lax
from jax.sharding import Mesh
from jax.sharding import PartitionSpec as P

COARSE_DEV = 32
DEV = ("dev_0", "dev_1")
GRP = ("grp_0", "grp_1", "grp_2")
GRP_DEV = ("grp_0", "grp_1", "grp_2", "dev_0", "dev_1")


def with_halo(x, sides, width):
    edges = {}
    for axis, dim in sides:
        peers, length = (lax.axis_size(axis), x.shape[dim])
        up = [(i, (i + 1) % peers) for i in range(peers)]
        last = lax.slice_in_dim(x, length - width, length, axis=dim)
        first = lax.slice_in_dim(x, 0, width, axis=dim)
        edges[dim] = (
            lax.ppermute(last, axis, up),
            lax.ppermute(first, axis, [(b, a) for a, b in up]),
        )
    done = []
    for _, dim in sides:
        low, high = edges[dim]
        around = [(width, width) if d in done else (0, 0) for d in range(x.ndim)]
        x = jnp.concatenate([jnp.pad(low, around), x, jnp.pad(high, around)], axis=dim)
        done.append(dim)
    return x


def by_axis(x, axes):
    for axis in axes:
        x = lax.psum(x, axis)
    return x


def cut_along(x, dim, peers):
    dims = x.shape
    pieces = x.reshape(*dims[:dim], peers, dims[dim] // peers, *dims[dim + 1 :])
    return jnp.moveaxis(pieces, dim, 0)


def sum_at_owner(x, axis, dim):
    peers = lax.axis_size(axis)
    pieces = lax.all_to_all(cut_along(x, dim, peers), axis, 0, 0, tiled=True)
    return jnp.sum(pieces, axis=0)


def coarse_tiles(own_a, nearby):
    block_count = own_a.shape[0]
    slot_count = nearby.shape[1]
    tile_size = nearby.shape[2]
    widened = jnp.transpose(nearby, (0, 2, 1, 3)).reshape(
        block_count + 2, tile_size, slot_count * tile_size
    )
    stacked = jnp.stack([widened[:-2], widened[1:-1], widened[2:]], axis=1)
    right_prod = jnp.einsum("bnij,bnjk->bnik", own_a, stacked, precision=lax.Precision.HIGHEST)
    right_prod = jnp.transpose(right_prod, (0, 2, 1, 3)).reshape(
        block_count, tile_size, 3 * slot_count * tile_size
    )
    left_prod = jnp.einsum(
        "bik,bic->bkc", widened[1:-1], right_prod, precision=lax.Precision.HIGHEST
    )
    left_prod = left_prod.reshape(block_count, slot_count, tile_size, 3 * slot_count, tile_size)
    return jnp.transpose(left_prod, (0, 1, 3, 2, 4))


def local(a_tiles, prolong, coarse_ids):
    fine_count = a_tiles.shape[0]
    tile_size = a_tiles.shape[-1]
    dev_count = lax.axis_size(DEV)
    grp_count = lax.axis_size(GRP)
    dev_index = lax.axis_index(DEV)
    coarse_grp = COARSE_DEV * dev_count
    ctiles = coarse_grp // tile_size
    nearby, nearby_ids = (
        with_halo(prolong, ((GRP_DEV, 0),), 1),
        with_halo(coarse_ids, ((GRP_DEV, 0),), 1),
    )
    position = jnp.arange(fine_count, dtype=jnp.int32)
    lower_win = jnp.where((position == 0) & (dev_index == 0), 0, 1).astype(jnp.int32)
    upper_win = jnp.where((position == fine_count - 1) & (dev_index == dev_count - 1), 2, 1).astype(
        jnp.int32
    )
    col_tiles = jnp.concatenate(
        [
            lower_win[:, None] * ctiles + nearby_ids[:-2],
            ctiles + coarse_ids,
            upper_win[:, None] * ctiles + nearby_ids[2:],
        ],
        axis=1,
    )
    products = coarse_tiles(a_tiles, nearby)
    partial_value = jnp.zeros((ctiles, 3 * ctiles, tile_size, tile_size), jnp.float32)
    partial_value = partial_value.at[coarse_ids[:, :, None], col_tiles[:, None, :]].add(products)
    partial_rows = jnp.transpose(partial_value, (0, 2, 1, 3)).reshape(coarse_grp, 3 * coarse_grp)
    own_trace = jnp.sum(jnp.diagonal(partial_rows[:, coarse_grp : 2 * coarse_grp]))
    trace_sum = by_axis(own_trace, GRP_DEV)
    middle_rows = sum_at_owner(partial_rows[:, coarse_grp : 2 * coarse_grp], DEV, 0)
    at_first = dev_index == 0
    at_last = dev_index == dev_count - 1
    edge_block = jnp.where(
        at_first,
        partial_rows[:, :coarse_grp],
        jnp.where(at_last, partial_rows[:, 2 * coarse_grp :], 0.0),
    )
    received = lax.all_to_all(edge_block, DEV, split_axis=0, concat_axis=0, tiled=True)
    lower_rows = received[:COARSE_DEV]
    upper_rows = received[(dev_count - 1) * COARSE_DEV :]
    owned_rows = jnp.concatenate([lower_rows, middle_rows, upper_rows], axis=1)
    mean_diag = trace_sum / (grp_count * coarse_grp)
    return owned_rows / mean_diag


def solution(mesh):
    torus = Mesh(mesh.devices.reshape(4, 2, 2, 4, 4), ("grp_0", "grp_1", "grp_2", "dev_0", "dev_1"))
    return jax.shard_map(
        local,
        mesh=torus,
        in_specs=(P(GRP_DEV, None, None, None), P(GRP_DEV, None, None, None), P(GRP_DEV, None)),
        out_specs=P(GRP_DEV, None),
        check_vma=False,
    )
```

profile of v0, /device:TPU:32, one launch (start us, length us, event | category | flops | bytes accessed | tf_op | source)
XLA Modules:
  0.0 308.0 jit_solution(531776822477899482)
XLA Ops:
  0.0 0.8 fusion.13
  0.8 1.6 collective-permute-start
  2.4 6.2 %collective-permute-start.1 = (s32[1,2]{0,1:T(2,128)S(1)}, s32[1,2]{0,1:T(2,128)S(1)}, u32[]{:S(2)}, u32[]{:S(2)}) collective-permute-start(s32[1,2]{0,1:T(2,128)S(1)} %get-tuple-element.19), channel_id=1, source_target_pairs={{1,0},{2,1},{3,2},{4,3},{5,4},{6,5},{7,6},{8,7},{9,8},{10,9},{11,1... | collective-permute-start | bytes 32 | tf_op jit(solution)/shard_map/ppermute | solution.py:22
  8.6 1.0 fusion.11
  9.6 0.1 collective-permute-start.2
  9.7 6.9 %collective-permute-start.3 = (f32[1,2,128,128]{3,2,1,0:T(8,128)S(1)}, f32[1,2,128,128]{3,2,1,0:T(8,128)S(1)}, u32[]{:S(2)}, u32[]{:S(2)}) collective-permute-start(f32[1,2,128,128]{3,2,1,0:T(8,128)S(1)} %get-tuple-element.9), channel_id=1, source_target_pairs={{1,0},{2,1},{3,2},{4,3},{5,4},{6,5},{7,6},{8,7},{9,8},{10,9},{11,1... | collective-permute-start | bytes 393224 | tf_op jit(solution)/shard_map/ppermute | solution.py:22
  16.5 0.7 clamp_shift-left_fusion.1
  17.2 0.7 clamp_compare_fusion.1
  17.9 0.1 copy.29
  18.0 0.1 copy.27
  18.1 0.0 collective-permute-done
  18.1 0.0 collective-permute-done.1
  18.1 0.8 pad_add_fusion
  18.9 0.1 slice_add_fusion
  19.1 0.1 copy.30
  19.1 0.1 copy.28
  19.2 0.1 or_select_fusion
  19.4 0.1 reshape.75
  19.5 3.2 %collective-permute-done.2 = f32[1,2,128,128]{3,2,1,0:T(8,128)S(1)} collective-permute-done((f32[1,2,128,128]{3,2,1,0:T(8,128)S(1)}, f32[1,2,128,128]{3,2,1,0:T(8,128)S(1)}, u32[]{:S(2)}, u32[]{:S(2)}) %collective-permute-start.2) | collective-permute-done | bytes 131104 | tf_op jit(solution)/shard_map/ppermute | solution.py:21
  22.8 2.5 maximum_bitcast_fusion
  25.3 4.7 %fusion.10 = (f32[32,128,2,128]{3,1,2,0:T(8,128)}, f32[32,128,2,128]{3,1,2,0:T(8,128)}, f32[32,128,2,128]{3,1,2,0:T(8,128)}) fusion(f32[34,128,2,128]{3,1,2,0:T(8,128)S(1)} %maximum_bitcast_fusion), kind=kLoop, calls=%fused_computation.33 | loop fusion | bytes 25165824 | tf_op jit(solution)/shard_map/slice | solution.py:58
  30.0 5.6 %copy.31 = f32[32,128,2,128]{1,3,2,0:T(8,128)} copy(f32[32,128,2,128]{3,1,2,0:T(8,128)} %get-tuple-element.7) | data formatting | bytes 8388608 | tf_op jit(solution)/shard_map/slice | solution.py:64
  35.6 5.6 %copy.32 = f32[32,128,2,128]{1,3,2,0:T(8,128)} copy(f32[32,128,2,128]{3,1,2,0:T(8,128)} %get-tuple-element.5) | data formatting | bytes 8388608 | tf_op jit(solution)/shard_map/slice | solution.py:58
  41.2 5.6 %copy.34 = f32[32,128,2,128]{1,3,2,0:T(8,128)} copy(f32[32,128,2,128]{3,1,2,0:T(8,128)} %get-tuple-element.6) | data formatting | bytes 8388608 | tf_op jit(solution)/shard_map/slice | solution.py:58
  46.8 15.3 %fusion = f32[32,3,256,128]{3,2,1,0:T(8,128)S(1)} fusion(f32[32,3,128,128]{3,2,1,0:T(8,128)} %param.3, f32[32,1,128,256]{2,3,1,0:T(8,128)} %bitcast.41, f32[32,1,128,256]{2,3,1,0:T(8,128)} %bitcast.37, f32[32,1,128,256]{2,3,1,0:T(8,128)} %bitcast.40), kind=kOutput, calls=%fused_computation.2 | convolution fusion | flops 4838129664 | bytes 31457280 | tf_op jit(solution)/shard_map/bnij,bnjk->bnik/dot_general | solution.py:59
  62.2 23.4 %fusion.14 = f32[32,256,768]{1,2,0:T(8,128)} fusion(f32[32,128,256]{1,2,0:T(8,128)S(1)} %bitcast.38, f32[32,128,768]{1,2,0:T(8,128)S(1)} %bitcast.35), kind=kOutput, calls=%fused_computation.37 | convolution fusion | flops 9663676416 | bytes 41943040 | tf_op jit(solution)/shard_map/bik,bic->bkc/dot_general | solution.py:63
  85.6 30.8 %reshape.66 = f32[32,2,128,6,128]{2,1,4,3,0:T(2,128)} reshape(f32[32,256,768]{1,2,0:T(8,128)} %fusion.14) | data formatting | bytes 50331648 | tf_op jit(solution)/shard_map/reshape | solution.py:66
  116.3 36.9 %copy.37 = f32[32,2,6,128,128]{4,3,2,1,0:T(8,128)} copy(f32[32,2,6,128,128]{3,1,4,2,0:T(2,128)} %bitcast.36) | data formatting | bytes 50331648 | tf_op jit(solution)/shard_map/transpose | solution.py:67
  153.2 0.4 broadcast_in_dim.35
  153.6 52.5 %scatter_fusion = f32[4,12,128,128]{3,2,1,0:T(8,128)S(1)} fusion(f32[4,12,128,128]{3,2,1,0:T(8,128)S(1)} %broadcast_in_dim.35, s32[384]{0:T(512)S(1)} %reshape.75, f32[384,128,128]{2,1,0:T(8,128)} %bitcast.34), kind=kCustom, calls=%fused_computation.1 | custom fusion | flops 6291456 | bytes 75500544 | tf_op jit(solution)/shard_map/scatter-add | solution.py:97
  206.1 2.8 copy.38
  208.9 2.2 copy.46
  211.1 0.3 fusion.12
  211.4 1.3 copy.39
  212.8 6.7 %all-to-all-start = ((f32[16,32,512]{2,1,0:T(8,128)}), f32[16,32,512]{2,1,0:T(8,128)S(1)}, u32[]{:S(2)}, u32[]{:S(2)}) async-start(f32[16,32,512]{2,1,0:T(8,128)} %bitcast.10), calls=%async_computation | async-start | bytes 2097152 | tf_op jit(solution)/shard_map/all_to_all | solution.py:109
  219.5 1.4 copy.43
  220.8 28.8 %all-to-all-done = f32[16,32,512]{2,1,0:T(8,128)S(1)} async-done(((f32[16,32,512]{2,1,0:T(8,128)}), f32[16,32,512]{2,1,0:T(8,128)S(1)}, u32[]{:S(2)}, u32[]{:S(2)}) %all-to-all-start) | async-done | bytes 1048608 | tf_op jit(solution)/shard_map/all_to_all | solution.py:109
  249.6 3.8 %all-to-all-start.1 = ((f32[16,32,512]{2,1,0:T(8,128)}), f32[16,32,512]{2,1,0:T(8,128)S(1)}, u32[]{:S(2)}, u32[]{:S(2)}) async-start(f32[16,32,512]{2,1,0:T(8,128)} %bitcast.12), calls=%async_computation.1 | async-start | bytes 2097152 | tf_op jit(solution)/shard_map/all_to_all | solution.py:47
  253.5 8.5 %gather_fusion = f32[512]{0:T(512)S(1)} fusion(f32[512,512]{1,0:T(8,128)} %copy.43, s32[512]{0:T(512)S(1)} %bitcast.39), kind=kCustom, calls=%fused_computation | custom fusion | bytes 8192 | tf_op jit(solution)/shard_map/jit(diagonal)/cond/branch_0_fun/gather | solution.py:99
  262.0 0.6 reduce_sum.19
  262.6 11.0 %psum.35 = f32[]{:T(128)} all-reduce(f32[]{:T(128)} %reduce_sum.19), channel_id=1, replica_groups=mesh['grp_0'=4,'grp_1'=2,'grp_2'=2,'dev_0'=4,'dev_1'=4] {'grp_0'}, use_global_device_ids=true, to_apply=%region_3.4 | all-reduce | flops 1 | bytes 8 | tf_op jit(solution)/shard_map/psum | solution.py:35
  273.6 5.5 %psum.36 = f32[]{:T(128)} all-reduce(f32[]{:T(128)} %psum.35), channel_id=1, replica_groups=mesh['grp_0'=4,'grp_1'=2,'grp_2'=2,'dev_0'=4,'dev_1'=4] {'grp_1'}, use_global_device_ids=true, to_apply=%region_4.5 | all-reduce | flops 1 | bytes 8 | tf_op jit(solution)/shard_map/psum | solution.py:35
  279.2 3.1 psum.37
  282.2 13.3 %psum.38 = f32[]{:T(128)} all-reduce(f32[]{:T(128)} %psum.37), channel_id=1, replica_groups=mesh['grp_0'=4,'grp_1'=2,'grp_2'=2,'dev_0'=4,'dev_1'=4] {'dev_0'}, use_global_device_ids=true, to_apply=%region_6.7 | all-reduce | flops 1 | bytes 8 | tf_op jit(solution)/shard_map/psum | solution.py:35
  295.5 11.0 %psum.39 = f32[]{:T(128)} all-reduce(f32[]{:T(128)} %psum.38), channel_id=1, replica_groups=mesh['grp_0'=4,'grp_1'=2,'grp_2'=2,'dev_0'=4,'dev_1'=4] {'dev_1'}, use_global_device_ids=true, to_apply=%region_7.8 | all-reduce | flops 1 | bytes 8 | tf_op jit(solution)/shard_map/psum | solution.py:35
  307.2 0.0 all-to-all-done.1
  307.2 0.1 reduce_sum.18
  307.3 0.7 maximum_divide_fusion
  (9 shorter events, 0.1 us)
Async XLA Ops:
  0.8 17.3 %collective-permute-start = (s32[1,2]{0,1:T(2,128)S(1)}, s32[1,2]{0,1:T(2,128)S(1)}, u32[]{:S(2)}, u32[]{:S(2)}) collective-permute-start(s32[1,2]{0,1:T(2,128)S(1)} %get-tuple-element.18), channel_id=1, source_target_pairs={{0,1},{1,2},{2,3},{3,4},{4,5},{5,6},{6,7},{7,8},{8,9},{9,10},{10,1... | collective-permute-start | bytes 32 | tf_op jit(solution)/shard_map/ppermute | solution.py:21
  2.4 15.7 %collective-permute-start.1 = (s32[1,2]{0,1:T(2,128)S(1)}, s32[1,2]{0,1:T(2,128)S(1)}, u32[]{:S(2)}, u32[]{:S(2)}) collective-permute-start(s32[1,2]{0,1:T(2,128)S(1)} %get-tuple-element.19), channel_id=1, source_target_pairs={{1,0},{2,1},{3,2},{4,3},{5,4},{6,5},{7,6},{8,7},{9,8},{10,9},{11,1... | collective-permute-start | bytes 32 | tf_op jit(solution)/shard_map/ppermute | solution.py:22
  9.6 13.2 %collective-permute-start.2 = (f32[1,2,128,128]{3,2,1,0:T(8,128)S(1)}, f32[1,2,128,128]{3,2,1,0:T(8,128)S(1)}, u32[]{:S(2)}, u32[]{:S(2)}) collective-permute-start(f32[1,2,128,128]{3,2,1,0:T(8,128)S(1)} %get-tuple-element.8), channel_id=1, source_target_pairs={{0,1},{1,2},{2,3},{3,4},{4,5},{5,6},{6,7},{7,8},{8,9},{9,10},{10,1... | collective-permute-start | bytes 393224 | tf_op jit(solution)/shard_map/ppermute | solution.py:21
  9.7 13.1 %collective-permute-start.3 = (f32[1,2,128,128]{3,2,1,0:T(8,128)S(1)}, f32[1,2,128,128]{3,2,1,0:T(8,128)S(1)}, u32[]{:S(2)}, u32[]{:S(2)}) collective-permute-start(f32[1,2,128,128]{3,2,1,0:T(8,128)S(1)} %get-tuple-element.9), channel_id=1, source_target_pairs={{1,0},{2,1},{3,2},{4,3},{5,4},{6,5},{7,6},{8,7},{9,8},{10,9},{11,1... | collective-permute-start | bytes 393224 | tf_op jit(solution)/shard_map/ppermute | solution.py:22
  46.8 15.3 %copy-start = (f32[32,128,2,128]{1,3,2,0:T(8,128)S(1)}, f32[32,128,2,128]{1,3,2,0:T(8,128)}, u32[]{:S(2)}) copy-start(f32[32,128,2,128]{1,3,2,0:T(8,128)} %copy.31) | copy-start | bytes 12582916
  212.8 36.9 %all-to-all-start = ((f32[16,32,512]{2,1,0:T(8,128)}), f32[16,32,512]{2,1,0:T(8,128)S(1)}, u32[]{:S(2)}, u32[]{:S(2)}) async-start(f32[16,32,512]{2,1,0:T(8,128)} %bitcast.10), calls=%async_computation | async-start | bytes 2097152 | tf_op jit(solution)/shard_map/all_to_all | solution.py:109
  249.6 57.6 %all-to-all-start.1 = ((f32[16,32,512]{2,1,0:T(8,128)}), f32[16,32,512]{2,1,0:T(8,128)S(1)}, u32[]{:S(2)}, u32[]{:S(2)}) async-start(f32[16,32,512]{2,1,0:T(8,128)} %bitcast.12), calls=%async_computation.1 | async-start | bytes 2097152 | tf_op jit(solution)/shard_map/all_to_all | solution.py:47
where the time goes:
time: 311 us; the launch traced here: 308 us
  local copies, waits for them, and re-layouts  108 us (35%)
  other arithmetic  59.1 us (19%)
  blocking collectives  44 us (14%)
  matrix products  38.7 us (12%)
  waiting for transfers between devices  32.1 us (10%)
  starting transfers between devices  25.2 us (8%)
    scatter-add x1, other arithmetic, local(): partial_value.at[coarse_ids[:, :, None], col_tiles[:, None, :]]  52.5 us
    psum x5, blocking collectives, by_axis(): x = lax.psum(x, axis)  44 us
    transpose x1, local copies, waits for them, and re-layouts, coarse_tiles(): return jnp.transpose(left_prod, (0, 1, 3, 2, 4))  36.9 us
    reshape x1, local copies, waits for them, and re-layouts, coarse_tiles(): left_prod.reshape(block_count, slot_count, tile_size, 3 * slot_count, til...  30.8 us
    all_to_all x1, waiting for transfers between devices, local(): lax.all_to_all(edge_block, DEV, split_axis=0, concat_axis=0, tiled=True)  28.8 us
    dot_general x1, matrix products, coarse_tiles(): jnp.einsum('bik,bic->bkc', widened[1:-1], right_prod, precision=lax.Preci...  23.4 us
    slice x3, local copies, waits for them, and re-layouts, coarse_tiles(): stacked = jnp.stack([widened[:-2], widened[1:-1], widened[2:]], axis=1)  16 us
    dot_general x1, matrix products, coarse_tiles(): jnp.einsum('bnij,bnjk->bnik', own_a, stacked, precision=lax.Precision.HIG...  15.3 us
  transfers between devices with their start and end apart: 6, of which 2 were waited for; matrix products, arithmetic and copies ran while one was open for 5% of the time, Pallas kernels for 0%

commit v1 on v0

--- a/solution.py
+++ b/solution.py
@@ -32,7 +32,7 @@
 
 def by_axis(x, axes):
     for axis in axes:
-        x = lax.psum(x, axis)
+        x = jnp.sum(jax.lax.all_gather(x, axis), axis=0)
     return x
 
 

time: 311 us -> 322 us (1.035)
  local copies, waits for them, and re-layouts: 108 us -> 119 us
    psum x5 -> x0, blocking collectives: 44 us -> none  [by_axis(): x = lax.psum(x, axis)]
    unnamed x0 -> x5, blocking collectives: none -> 40.8 us
    unnamed x4 -> x29, local copies, waits for them, and re-layouts: 3.57 us -> 14.1 us
  transfers between devices with their start and end apart: 6 -> 6, of which waited for: 2 -> 2; matrix products, arithmetic and copies ran while one was open for 5% -> 9% of each run, Pallas kernels for 0% -> 0%
where the time goes in v1:
time: 322 us; the launch traced here: 319 us
  local copies, waits for them, and re-layouts  119 us (37%)
  other arithmetic  62.2 us (19%)
  blocking collectives  40.8 us (13%)
  matrix products  38.7 us (12%)
  waiting for transfers between devices  32.1 us (10%)
  starting transfers between devices  25.3 us (8%)
    scatter-add x1, other arithmetic, local(): partial_value.at[coarse_ids[:, :, None], col_tiles[:, None, :]]  52.5 us
    unnamed x5, blocking collectives  40.8 us
    transpose x1, local copies, waits for them, and re-layouts, coarse_tiles(): return jnp.transpose(left_prod, (0, 1, 3, 2, 4))  36.9 us
    reshape x1, local copies, waits for them, and re-layouts, coarse_tiles(): left_prod.reshape(block_count, slot_count, tile_size, 3 * slot_count, til...  30.8 us
    all_to_all x1, waiting for transfers between devices, local(): lax.all_to_all(edge_block, DEV, split_axis=0, concat_axis=0, tiled=True)  28.8 us
    dot_general x1, matrix products, coarse_tiles(): jnp.einsum('bik,bic->bkc', widened[1:-1], right_prod, precision=lax.Preci...  23.4 us
    slice x3, local copies, waits for them, and re-layouts, coarse_tiles(): stacked = jnp.stack([widened[:-2], widened[1:-1], widened[2:]], axis=1)  16 us
    dot_general x1, matrix products, coarse_tiles(): jnp.einsum('bnij,bnjk->bnik', own_a, stacked, precision=lax.Precision.HIG...  15.3 us
  transfers between devices with their start and end apart: 6, of which 2 were waited for; matrix products, arithmetic and copies ran while one was open for 9% of the time, Pallas kernels for 0%

profile of v1, /device:TPU:32, one launch (start us, length us, event | category | flops | bytes accessed | tf_op | source)
XLA Modules:
  0.0 318.5 jit_solution(6943979599259169452)
XLA Ops:
  0.0 0.8 fusion.13
  0.8 1.6 collective-permute-start
  2.4 6.2 %collective-permute-start.1 = (s32[1,2]{0,1:T(2,128)S(1)}, s32[1,2]{0,1:T(2,128)S(1)}, u32[]{:S(2)}, u32[]{:S(2)}) collective-permute-start(s32[1,2]{0,1:T(2,128)S(1)} %get-tuple-element.19), channel_id=1, source_target_pairs={{1,0},{2,1},{3,2},{4,3},{5,4},{6,5},{7,6},{8,7},{9,8},{10,9},{11,1... | collective-permute-start | bytes 32 | tf_op jit(solution)/shard_map/ppermute | solution.py:22
  8.6 1.0 fusion.11
  9.7 6.9 %collective-permute-start.3 = (f32[1,2,128,128]{3,2,1,0:T(8,128)S(1)}, f32[1,2,128,128]{3,2,1,0:T(8,128)S(1)}, u32[]{:S(2)}, u32[]{:S(2)}) collective-permute-start(f32[1,2,128,128]{3,2,1,0:T(8,128)S(1)} %get-tuple-element.9), channel_id=1, source_target_pairs={{1,0},{2,1},{3,2},{4,3},{5,4},{6,5},{7,6},{8,7},{9,8},{10,9},{11,1... | collective-permute-start | bytes 393224 | tf_op jit(solution)/shard_map/ppermute | solution.py:22
  16.5 0.7 clamp_shift-left_fusion.1
  17.2 0.7 clamp_compare_fusion.1
  18.1 0.8 pad_add_fusion
  19.5 3.2 %collective-permute-done.2 = f32[1,2,128,128]{3,2,1,0:T(8,128)S(1)} collective-permute-done((f32[1,2,128,128]{3,2,1,0:T(8,128)S(1)}, f32[1,2,128,128]{3,2,1,0:T(8,128)S(1)}, u32[]{:S(2)}, u32[]{:S(2)}) %collective-permute-start.2) | collective-permute-done | bytes 131104 | tf_op jit(solution)/shard_map/ppermute | solution.py:21
  22.8 2.5 maximum_bitcast_fusion
  25.3 4.7 %fusion.10 = (f32[32,128,2,128]{3,1,2,0:T(8,128)}, f32[32,128,2,128]{3,1,2,0:T(8,128)}, f32[32,128,2,128]{3,1,2,0:T(8,128)}) fusion(f32[34,128,2,128]{3,1,2,0:T(8,128)S(1)} %maximum_bitcast_fusion), kind=kLoop, calls=%fused_computation.33 | loop fusion | bytes 25165824 | tf_op jit(solution)/shard_map/slice | solution.py:58
  30.0 5.6 %copy.31 = f32[32,128,2,128]{1,3,2,0:T(8,128)} copy(f32[32,128,2,128]{3,1,2,0:T(8,128)} %get-tuple-element.7) | data formatting | bytes 8388608 | tf_op jit(solution)/shard_map/slice | solution.py:64
  35.6 5.6 %copy.32 = f32[32,128,2,128]{1,3,2,0:T(8,128)} copy(f32[32,128,2,128]{3,1,2,0:T(8,128)} %get-tuple-element.5) | data formatting | bytes 8388608 | tf_op jit(solution)/shard_map/slice | solution.py:58
  41.2 5.6 %copy.34 = f32[32,128,2,128]{1,3,2,0:T(8,128)} copy(f32[32,128,2,128]{3,1,2,0:T(8,128)} %get-tuple-element.6) | data formatting | bytes 8388608 | tf_op jit(solution)/shard_map/slice | solution.py:58
  46.8 15.3 %fusion = f32[32,3,256,128]{3,2,1,0:T(8,128)S(1)} fusion(f32[32,3,128,128]{3,2,1,0:T(8,128)} %param.3, f32[32,1,128,256]{2,3,1,0:T(8,128)} %bitcast.51, f32[32,1,128,256]{2,3,1,0:T(8,128)} %bitcast.47, f32[32,1,128,256]{2,3,1,0:T(8,128)} %bitcast.50), kind=kOutput, calls=%fused_computation.2 | convolution fusion | flops 4838129664 | bytes 31457280 | tf_op jit(solution)/shard_map/bnij,bnjk->bnik/dot_general | solution.py:59
  62.2 23.4 %fusion.14 = f32[32,256,768]{1,2,0:T(8,128)} fusion(f32[32,128,256]{1,2,0:T(8,128)S(1)} %bitcast.48, f32[32,128,768]{1,2,0:T(8,128)S(1)} %bitcast.45), kind=kOutput, calls=%fused_computation.37 | convolution fusion | flops 9663676416 | bytes 41943040 | tf_op jit(solution)/shard_map/bik,bic->bkc/dot_general | solution.py:63
  85.6 30.8 %reshape.66 = f32[32,2,128,6,128]{2,1,4,3,0:T(2,128)} reshape(f32[32,256,768]{1,2,0:T(8,128)} %fusion.14) | data formatting | bytes 50331648 | tf_op jit(solution)/shard_map/reshape | solution.py:66
  116.3 36.9 %copy.37 = f32[32,2,6,128,128]{4,3,2,1,0:T(8,128)} copy(f32[32,2,6,128,128]{3,1,4,2,0:T(2,128)} %bitcast.46) | data formatting | bytes 50331648 | tf_op jit(solution)/shard_map/transpose | solution.py:67
  153.6 52.5 %scatter_fusion = f32[4,12,128,128]{3,2,1,0:T(8,128)S(1)} fusion(f32[4,12,128,128]{3,2,1,0:T(8,128)S(1)} %broadcast_in_dim.35, s32[384]{0:T(512)S(1)} %reshape.75, f32[384,128,128]{2,1,0:T(8,128)} %bitcast.44), kind=kCustom, calls=%fused_computation.1 | custom fusion | flops 6291456 | bytes 75500544 | tf_op jit(solution)/shard_map/scatter-add | solution.py:97
  206.1 2.8 copy.38
  208.9 2.2 copy.46
  211.4 1.4 copy.39
  212.8 6.8 %all-to-all-start = ((f32[16,32,512]{2,1,0:T(8,128)}), f32[16,32,512]{2,1,0:T(8,128)S(1)}, u32[]{:S(2)}, u32[]{:S(2)}) async-start(f32[16,32,512]{2,1,0:T(8,128)} %bitcast.10), calls=%async_computation | async-start | bytes 2097152 | tf_op jit(solution)/shard_map/all_to_all | solution.py:109
  219.7 1.3 copy.43
  221.0 28.8 %all-to-all-done = f32[16,32,512]{2,1,0:T(8,128)S(1)} async-done(((f32[16,32,512]{2,1,0:T(8,128)}), f32[16,32,512]{2,1,0:T(8,128)S(1)}, u32[]{:S(2)}, u32[]{:S(2)}) %all-to-all-start) | async-done | bytes 1048608 | tf_op jit(solution)/shard_map/all_to_all | solution.py:109
  249.8 3.8 %all-to-all-start.1 = ((f32[16,32,512]{2,1,0:T(8,128)}), f32[16,32,512]{2,1,0:T(8,128)S(1)}, u32[]{:S(2)}, u32[]{:S(2)}) async-start(f32[16,32,512]{2,1,0:T(8,128)} %bitcast.12), calls=%async_computation.1 | async-start | bytes 2097152 | tf_op jit(solution)/shard_map/all_to_all | solution.py:47
  253.7 0.7 dynamic-slice
  254.3 8.4 %gather_fusion = f32[512]{0:T(512)S(1)} fusion(f32[512,512]{1,0:T(8,128)} %copy.43, s32[512]{0:T(512)S(1)} %bitcast.49), kind=kCustom, calls=%fused_computation | custom fusion | bytes 8192 | tf_op jit(solution)/shard_map/jit(diagonal)/cond/branch_0_fun/gather | solution.py:99
  263.4 1.4 dynamic-update-slice
  264.8 0.7 dynamic-slice.1
  265.5 10.4 %all-reduce = f32[4]{0:T(128)S(1)} all-reduce(f32[4]{0:T(128)S(1)} %dynamic-update-slice), channel_id=1, replica_groups=mesh['grp_0'=4,'grp_1'=2,'grp_2'=2,'dev_0'=4,'dev_1'=4] {'grp_0'}, use_global_device_ids=true, to_apply=%add | all-reduce | flops 4 | bytes 32
  275.9 0.6 reduce_sum.65
  276.5 1.4 dynamic-update-slice.1
  277.9 0.7 dynamic-slice.2
  278.6 4.9 %all-reduce.1 = f32[2]{0:T(128)S(1)} all-reduce(f32[2]{0:T(128)S(1)} %dynamic-update-slice.1), channel_id=1, replica_groups=mesh['grp_0'=4,'grp_1'=2,'grp_2'=2,'dev_0'=4,'dev_1'=4] {'grp_1'}, use_global_device_ids=true, to_apply=%add.1 | all-reduce | flops 2 | bytes 16
  283.5 0.6 reduce_sum.66
  284.1 1.4 dynamic-update-slice.2
  285.6 0.7 dynamic-slice.3
  286.2 2.4 all-reduce.2
  288.7 0.6 reduce_sum.67
  289.3 1.4 dynamic-update-slice.3
  290.7 0.7 dynamic-slice.4
  291.4 12.6 %all-reduce.3 = f32[4]{0:T(128)S(1)} all-reduce(f32[4]{0:T(128)S(1)} %dynamic-update-slice.3), channel_id=1, replica_groups=mesh['grp_0'=4,'grp_1'=2,'grp_2'=2,'dev_0'=4,'dev_1'=4] {'dev_0'}, use_global_device_ids=true, to_apply=%add.3 | all-reduce | flops 4 | bytes 32
  304.0 0.6 reduce_sum.68
  304.6 1.4 dynamic-update-slice.4
  306.1 10.4 %all-reduce.4 = f32[4]{0:T(128)S(1)} all-reduce(f32[4]{0:T(128)S(1)} %dynamic-update-slice.4), channel_id=1, replica_groups=mesh['grp_0'=4,'grp_1'=2,'grp_2'=2,'dev_0'=4,'dev_1'=4] {'dev_1'}, use_global_device_ids=true, to_apply=%add.4 | all-reduce | flops 4 | bytes 32
  316.4 0.6 reduce_sum.69
  317.8 0.7 maximum_divide_fusion
  (39 shorter events, 2.3 us)
Async XLA Ops:
  0.8 17.3 %collective-permute-start = (s32[1,2]{0,1:T(2,128)S(1)}, s32[1,2]{0,1:T(2,128)S(1)}, u32[]{:S(2)}, u32[]{:S(2)}) collective-permute-start(s32[1,2]{0,1:T(2,128)S(1)} %get-tuple-element.18), channel_id=1, source_target_pairs={{0,1},{1,2},{2,3},{3,4},{4,5},{5,6},{6,7},{7,8},{8,9},{9,10},{10,1... | collective-permute-start | bytes 32 | tf_op jit(solution)/shard_map/ppermute | solution.py:21
  2.4 15.7 %collective-permute-start.1 = (s32[1,2]{0,1:T(2,128)S(1)}, s32[1,2]{0,1:T(2,128)S(1)}, u32[]{:S(2)}, u32[]{:S(2)}) collective-permute-start(s32[1,2]{0,1:T(2,128)S(1)} %get-tuple-element.19), channel_id=1, source_target_pairs={{1,0},{2,1},{3,2},{4,3},{5,4},{6,5},{7,6},{8,7},{9,8},{10,9},{11,1... | collective-permute-start | bytes 32 | tf_op jit(solution)/shard_map/ppermute | solution.py:22
  9.6 13.2 %collective-permute-start.2 = (f32[1,2,128,128]{3,2,1,0:T(8,128)S(1)}, f32[1,2,128,128]{3,2,1,0:T(8,128)S(1)}, u32[]{:S(2)}, u32[]{:S(2)}) collective-permute-start(f32[1,2,128,128]{3,2,1,0:T(8,128)S(1)} %get-tuple-element.8), channel_id=1, source_target_pairs={{0,1},{1,2},{2,3},{3,4},{4,5},{5,6},{6,7},{7,8},{8,9},{9,10},{10,1... | collective-permute-start | bytes 393224 | tf_op jit(solution)/shard_map/ppermute | solution.py:21
  9.7 13.1 %collective-permute-start.3 = (f32[1,2,128,128]{3,2,1,0:T(8,128)S(1)}, f32[1,2,128,128]{3,2,1,0:T(8,128)S(1)}, u32[]{:S(2)}, u32[]{:S(2)}) collective-permute-start(f32[1,2,128,128]{3,2,1,0:T(8,128)S(1)} %get-tuple-element.9), channel_id=1, source_target_pairs={{1,0},{2,1},{3,2},{4,3},{5,4},{6,5},{7,6},{8,7},{9,8},{10,9},{11,1... | collective-permute-start | bytes 393224 | tf_op jit(solution)/shard_map/ppermute | solution.py:22
  46.8 15.3 %copy-start = (f32[32,128,2,128]{1,3,2,0:T(8,128)S(1)}, f32[32,128,2,128]{1,3,2,0:T(8,128)}, u32[]{:S(2)}) copy-start(f32[32,128,2,128]{1,3,2,0:T(8,128)} %copy.31) | copy-start | bytes 12582916
  211.4 42.2 %copy-start.5 = (u32[256]{0:T(256)S(1)}, u32[256]{0:T(256)}, u32[]{:S(2)}) copy-start(u32[256]{0:T(256)} %constant.72) | copy-start | bytes 3076
  212.8 52.0 %copy-start.4 = (u32[256]{0:T(256)S(1)}, u32[256]{0:T(256)}, u32[]{:S(2)}) copy-start(u32[256]{0:T(256)} %constant.77) | copy-start | bytes 3076
  212.8 65.1 %copy-start.3 = (u32[256]{0:T(256)S(1)}, u32[256]{0:T(256)}, u32[]{:S(2)}) copy-start(u32[256]{0:T(256)} %constant.82) | copy-start | bytes 3076
  212.8 72.7 %copy-start.2 = (u32[256]{0:T(256)S(1)}, u32[256]{0:T(256)}, u32[]{:S(2)}) copy-start(u32[256]{0:T(256)} %constant.87) | copy-start | bytes 3076
  212.8 77.9 %copy-start.1 = (u32[256]{0:T(256)S(1)}, u32[256]{0:T(256)}, u32[]{:S(2)}) copy-start(u32[256]{0:T(256)} %constant.92) | copy-start | bytes 3076
  212.8 37.0 %all-to-all-start = ((f32[16,32,512]{2,1,0:T(8,128)}), f32[16,32,512]{2,1,0:T(8,128)S(1)}, u32[]{:S(2)}, u32[]{:S(2)}) async-start(f32[16,32,512]{2,1,0:T(8,128)} %bitcast.10), calls=%async_computation | async-start | bytes 2097152 | tf_op jit(solution)/shard_map/all_to_all | solution.py:109
  249.8 67.9 %all-to-all-start.1 = ((f32[16,32,512]{2,1,0:T(8,128)}), f32[16,32,512]{2,1,0:T(8,128)S(1)}, u32[]{:S(2)}, u32[]{:S(2)}) async-start(f32[16,32,512]{2,1,0:T(8,128)} %bitcast.12), calls=%async_computation.1 | async-start | bytes 2097152 | tf_op jit(solution)/shard_map/all_to_all | solution.py:47
